TPU v7x, 32 devices: a 4x4x1 block of a 4x4x8 slice. The times are simulated.
32 devices in a mesh: batch: 1 (over z), row: 4 (over y), col: 8 (over x, core).
Axes of the slice: x: 4, y: 4, z: 1, core: 2. Of those that a mesh axis runs over, the one named last changes fastest.
The devices are a block of a 4x4x8 slice.
Arguments:
- left_op: bfloat16 [16384, 16384], P(('batch', 'row'), 'col')
- left_start: float32 [16384, 256], P(('batch', 'row', 'col'))
- right_op: bfloat16 [16384, 16384], P(('batch', 'row'), 'col')
- right_start: float32 [16384, 256], P(('batch', 'row', 'col'))
Outputs:
- output 1: float32 [16384, 256], P(('batch', 'row', 'col'))
- output 2: float32 [256, 256], P('batch')
- output 3: float32 [16384, 256], P(('batch', 'row', 'col'))
- output 4: float32 [256, 256], P('batch')
All inputs are finite; a program needn't handle non-finite values.
Results may differ from a plain program's by a relative error of at most 0.001.
Values are sent between devices in bfloat16 or wider.
A program may use at most 768 MiB of HBM per device.

v0:
```python
import jax
import jax.numpy as jnp
from jax import lax
from jax.sharding import PartitionSpec as P

SWEEPS = 4
ROW_CONTRACT = (((0,), (0,)), ((), ()))


def gram_total(lhs_mat, rhs_mat, precision, grid_axes):
    local_gram = lax.dot_general(lhs_mat, rhs_mat, ROW_CONTRACT, precision=precision, preferred_element_type=jnp.float32)
    return lax.psum(local_gram, grid_axes)


def cholqr_step(y_mat, gram_mat):
    chol_low = jnp.linalg.cholesky(gram_mat)
    return lax.linalg.triangular_solve(chol_low, y_mat, left_side=False, lower=True, transpose_a=True)


def orthonormalize(y_sub, total_rows, grid_axes):
    y_half = y_sub.astype(jnp.bfloat16)
    gram_one = gram_total(y_half, y_half, None, grid_axes) / total_rows
    y_one = cholqr_step(y_sub, gram_one)
    gram_two = gram_total(y_one, y_one, lax.Precision.HIGHEST, grid_axes) / total_rows
    return cholqr_step(y_one, gram_two)


def solution(mesh):
    row_size = mesh.shape["row"]
    col_size = mesh.shape["col"]
    grid_axes = ("row", "col")
    perm_pairs = [(src_index, (src_index % row_size) * col_size + src_index // row_size) for src_index in range(row_size * col_size)]

    def apply_op(op_blk, x_sub):
        x_moved = lax.ppermute(x_sub.astype(jnp.bfloat16), grid_axes, perm_pairs)
        x_col = lax.all_gather(x_moved, "row", axis=0, tiled=True)
        partial_prod = jnp.dot(op_blk, x_col, preferred_element_type=jnp.float32)
        return lax.psum_scatter(partial_prod, "col", scatter_dimension=0, tiled=True)

    def iterate_local(op_blk, start_sub):
        total_rows = op_blk.shape[0] * row_size
        x_sub = start_sub
        for sweep_index in range(SWEEPS):
            x_sub = orthonormalize(apply_op(op_blk, x_sub), total_rows, grid_axes)
        z_sub = apply_op(op_blk, x_sub)
        rayleigh = gram_total(x_sub, z_sub, lax.Precision.HIGHEST, grid_axes) / total_rows
        return x_sub, rayleigh

    def local_program(left_op, left_start, right_op, right_start):
        left_basis, left_rayleigh = iterate_local(left_op, left_start)
        right_basis, right_rayleigh = iterate_local(right_op, right_start)
        return left_basis, left_rayleigh, right_basis, right_rayleigh

    op_spec = P(("batch", "row"), "col")
    vec_spec = P(("batch", "row", "col"), None)
    small_spec = P("batch", None)
    return jax.shard_map(local_program, mesh=mesh, in_specs=(op_spec, vec_spec, op_spec, vec_spec), out_specs=(vec_spec, small_spec, vec_spec, small_spec), check_vma=False)
```

profile of v0, /device:TPU:97, one launch (start us, length us, event | category | flops | bytes accessed | tf_op | source)
XLA Modules:
  0.0 2537.8 jit_solution(10143315796256302417)
XLA Ops:
  31.0 13.1 collective-permute-done
  52.8 12.5 fusion.241
  76.2 12.5 fusion.240
  88.9 24.8 reduce-scatter.21.cloned.1.call-done
  115.9 34.3 %reduce-scatter.11.cloned.1.call-done = f32[512,256]{1,0:T(8,128)} async-done(((f32[4096,256]{1,0:T(8,128)}), f32[512,256]{1,0:T(8,128)}) %reduce-scatter.11.cloned.1.call-update) | async-done | bytes 524304 | tf_op jit(solution)/shard_map/reduce_scatter | solution.py:38
  152.6 97.1 %all-reduce.36.cloned.1.call-done = (f32[256,256]{0,1:T(8,128)}, f32[256,256]{0,1:T(8,128)}) async-done(((f32[256,256]{0,1:T(8,128)}, f32[256,256]{0,1:T(8,128)}), (f32[256,256]{0,1:T(8,128)}, f32[256,256]{0,1:T(8,128)})) %all-reduce.36.cloned.1.call-update) | async-done | bytes 524304 | tf_op jit(solution)/shard_map/psum | solution.py:12
  253.1 11.7 cholesky.990
  275.2 11.7 cholesky.1007
  293.6 20.1 custom-call.58
  315.7 11.7 cholesky.718
  337.8 11.7 cholesky.735
  356.2 19.9 custom-call.42
  383.5 93.7 %all-reduce.34.cloned.1.call-done = (f32[256,256]{0,1:T(8,128)}, f32[256,256]{0,1:T(8,128)}) async-done(((f32[256,256]{0,1:T(8,128)}, f32[256,256]{0,1:T(8,128)}), (f32[256,256]{0,1:T(8,128)}, f32[256,256]{0,1:T(8,128)})) %all-reduce.34.cloned.1.call-update) | async-done | bytes 524304 | tf_op jit(solution)/shard_map/psum | solution.py:12
  501.4 11.7 cholesky.1041
  519.8 19.7 custom-call.60
  568.1 11.7 cholesky.769
  587.6 19.7 custom-call.44
  623.9 12.6 convolution_bitcast_fusion.3
  645.1 12.6 convolution_bitcast_fusion.7
  658.1 24.6 reduce-scatter.23.cloned.1.call-done
  684.8 34.2 %reduce-scatter.13.cloned.1.call-done = f32[512,256]{0,1:T(8,128)} async-done(((f32[4096,256]{0,1:T(8,128)}), f32[512,256]{0,1:T(8,128)}) %reduce-scatter.13.cloned.1.call-update) | async-done | bytes 524304 | tf_op jit(solution)/shard_map/reduce_scatter | solution.py:38
  721.4 97.4 %all-reduce.32.cloned.1.call-done = (f32[256,256]{0,1:T(8,128)}, f32[256,256]{0,1:T(8,128)}) async-done(((f32[256,256]{0,1:T(8,128)}, f32[256,256]{0,1:T(8,128)}), (f32[256,256]{0,1:T(8,128)}, f32[256,256]{0,1:T(8,128)})) %all-reduce.32.cloned.1.call-update) | async-done | bytes 524304 | tf_op jit(solution)/shard_map/psum | solution.py:12
  843.0 11.7 cholesky.1075
  861.4 20.1 custom-call.62
  907.5 11.7 cholesky.803
  925.9 19.9 custom-call.46
  953.0 93.7 %all-reduce.30.cloned.1.call-done = (f32[256,256]{0,1:T(8,128)}, f32[256,256]{0,1:T(8,128)}) async-done(((f32[256,256]{0,1:T(8,128)}, f32[256,256]{0,1:T(8,128)}), (f32[256,256]{0,1:T(8,128)}, f32[256,256]{0,1:T(8,128)})) %all-reduce.30.cloned.1.call-update) | async-done | bytes 524304 | tf_op jit(solution)/shard_map/psum | solution.py:12
  1070.9 11.7 cholesky.1109
  1089.7 19.7 custom-call.64
  1137.6 11.7 cholesky.837
  1157.1 19.7 custom-call.48
  1193.5 12.6 convolution_bitcast_fusion.2
  1214.7 12.6 convolution_bitcast_fusion.6
  1227.6 24.4 reduce-scatter.25.cloned.1.call-done
  1254.2 34.3 %reduce-scatter.15.cloned.1.call-done = f32[512,256]{0,1:T(8,128)} async-done(((f32[4096,256]{0,1:T(8,128)}), f32[512,256]{0,1:T(8,128)}) %reduce-scatter.15.cloned.1.call-update) | async-done | bytes 524304 | tf_op jit(solution)/shard_map/reduce_scatter | solution.py:38
  1290.7 97.3 %all-reduce.28.cloned.1.call-done = (f32[256,256]{0,1:T(8,128)}, f32[256,256]{0,1:T(8,128)}) async-done(((f32[256,256]{0,1:T(8,128)}, f32[256,256]{0,1:T(8,128)}), (f32[256,256]{0,1:T(8,128)}, f32[256,256]{0,1:T(8,128)})) %all-reduce.28.cloned.1.call-update) | async-done | bytes 524304 | tf_op jit(solution)/shard_map/psum | solution.py:12
  1412.2 11.7 cholesky.1143
  1430.6 20.1 custom-call.66
  1476.7 11.7 cholesky.871
  1495.1 19.9 custom-call.50
  1522.2 93.7 %all-reduce.26.cloned.1.call-done = (f32[256,256]{0,1:T(8,128)}, f32[256,256]{0,1:T(8,128)}) async-done(((f32[256,256]{0,1:T(8,128)}, f32[256,256]{0,1:T(8,128)}), (f32[256,256]{0,1:T(8,128)}, f32[256,256]{0,1:T(8,128)})) %all-reduce.26.cloned.1.call-update) | async-done | bytes 524304 | tf_op jit(solution)/shard_map/psum | solution.py:12
  1640.1 11.7 cholesky.1177
  1658.9 19.7 custom-call.68
  1706.8 11.7 cholesky.905
  1726.3 19.7 custom-call.52
  1762.7 12.6 convolution_bitcast_fusion.1
  1783.9 12.6 convolution_bitcast_fusion.5
  1796.8 24.5 reduce-scatter.27.cloned.1.call-done
  1823.5 34.5 %reduce-scatter.17.cloned.1.call-done = f32[512,256]{0,1:T(8,128)} async-done(((f32[4096,256]{0,1:T(8,128)}), f32[512,256]{0,1:T(8,128)}) %reduce-scatter.17.cloned.1.call-update) | async-done | bytes 524304 | tf_op jit(solution)/shard_map/reduce_scatter | solution.py:38
  1860.3 97.6 %all-reduce.24.cloned.1.call-done = (f32[256,256]{0,1:T(8,128)}, f32[256,256]{0,1:T(8,128)}) async-done(((f32[256,256]{0,1:T(8,128)}, f32[256,256]{0,1:T(8,128)}), (f32[256,256]{0,1:T(8,128)}, f32[256,256]{0,1:T(8,128)})) %all-reduce.24.cloned.1.call-update) | async-done | bytes 524304 | tf_op jit(solution)/shard_map/psum | solution.py:12
  1982.0 11.7 cholesky.1211
  2000.4 20.1 custom-call.70
  2046.5 11.7 cholesky.939
  2064.9 19.9 custom-call.54
  2092.1 93.7 %all-reduce.22.cloned.1.call-done = (f32[256,256]{0,1:T(8,128)}, f32[256,256]{0,1:T(8,128)}) async-done(((f32[256,256]{0,1:T(8,128)}, f32[256,256]{0,1:T(8,128)}), (f32[256,256]{0,1:T(8,128)}, f32[256,256]{0,1:T(8,128)})) %all-reduce.22.cloned.1.call-update) | async-done | bytes 524304 | tf_op jit(solution)/shard_map/psum | solution.py:12
  2210.0 11.7 cholesky.1245
  2228.8 19.7 custom-call.72
  2276.7 11.7 cholesky.973
  2296.1 19.7 custom-call.56
  2332.5 12.6 convolution_bitcast_fusion
  2353.6 12.6 convolution_bitcast_fusion.4
  2366.4 24.5 reduce-scatter.29.cloned.1.call-done
  2393.3 34.3 %reduce-scatter.19.cloned.1.call-done = f32[512,256]{0,1:T(8,128)} async-done(((f32[4096,256]{0,1:T(8,128)}), f32[512,256]{0,1:T(8,128)}) %reduce-scatter.19.cloned.1.call-update) | async-done | bytes 524304 | tf_op jit(solution)/shard_map/reduce_scatter | solution.py:38
  2432.1 95.4 %all-reduce.20.cloned.1.call-done = (f32[256,256]{0,1:T(8,128)}, f32[256,256]{0,1:T(8,128)}) async-done(((f32[256,256]{0,1:T(8,128)}, f32[256,256]{0,1:T(8,128)}), (f32[256,256]{0,1:T(8,128)}, f32[256,256]{0,1:T(8,128)})) %all-reduce.20.cloned.1.call-update) | async-done | bytes 524304 | tf_op jit(solution)/shard_map/psum | solution.py:12
  (542 shorter events, 743.5 us)
Async XLA Ops:
  7.2 45.6 %all-gather.21.cloned.1.call-start = ((), (), s32[]{:S(2)}) async-start(), calls=%async_computation.20 | async-start | bytes 1310720 | tf_op jit(solution)/shard_map/all_gather | solution.py:36
  8.3 16.3 collective-permute-start.5
  24.6 0.7 copy-start.4
  25.4 50.9 %all-gather.11.cloned.1.call-start = ((), (), s32[]{:S(2)}) async-start(), calls=%async_computation.10 | async-start | bytes 1310720 | tf_op jit(solution)/shard_map/all_gather | solution.py:36
  26.5 17.5 collective-permute-start
  44.0 0.7 copy-start.5
  44.8 68.9 %reduce-scatter.21.cloned.1.call-start = ((), (), s32[]{:S(2)}) async-start(), calls=%async_computation.21 | async-start | bytes 4718592 | tf_op jit(solution)/shard_map/reduce_scatter | solution.py:38
  65.3 84.8 %reduce-scatter.11.cloned.1.call-start = ((), (), s32[]{:S(2)}) async-start(), calls=%async_computation.11 | async-start | bytes 4718592 | tf_op jit(solution)/shard_map/reduce_scatter | solution.py:38
  88.8 160.9 %all-reduce.36.cloned.1.call-start = ((), (), s32[]{:S(2)}) async-start(), calls=%async_computation.38 | async-start | bytes 1048576 | tf_op jit(solution)/shard_map/psum | solution.py:12
  152.4 324.8 %all-reduce.34.cloned.1.call-start = ((), (), s32[]{:S(2)}) async-start(), calls=%async_computation.37 | async-start | bytes 1048576 | tf_op jit(solution)/shard_map/psum | solution.py:12
  383.4 240.5 %all-gather.23.cloned.1.call-start = ((), (), s32[]{:S(2)}) async-start(), calls=%async_computation.22 | async-start | bytes 1310720 | tf_op jit(solution)/shard_map/all_gather | solution.py:36
  540.7 41.7 %collective-permute-start.6 = (bf16[512,256]{0,1:T(8,128)(2,1)S(1)}, bf16[512,256]{0,1:T(8,128)(2,1)S(1)}, u32[]{:S(2)}, u32[]{:S(2)}) collective-permute-start(bf16[512,256]{0,1:T(8,128)(2,1)S(1)} %maximum_convert_fusion.3), channel_id=1, source_target_pairs={{0,0},{1,8},{2,16},{3,24},{4,1},{5,9},{6,17},{7,25},{8,2},{9,10},{... | collective-permute-start | bytes 786440 | tf_op jit(solution)/shard_map/ppermute | solution.py:35
  582.5 0.7 copy-start.1
  583.2 61.9 %all-gather.13.cloned.1.call-start = ((), (), s32[]{:S(2)}) async-start(), calls=%async_computation.12 | async-start | bytes 1310720 | tf_op jit(solution)/shard_map/all_gather | solution.py:36
  608.6 14.5 collective-permute-start.1
  623.1 0.7 copy-start.6
  623.8 58.8 %reduce-scatter.23.cloned.1.call-start = ((), (), s32[]{:S(2)}) async-start(), calls=%async_computation.23 | async-start | bytes 4718592 | tf_op jit(solution)/shard_map/reduce_scatter | solution.py:38
  636.6 82.5 %reduce-scatter.13.cloned.1.call-start = ((), (), s32[]{:S(2)}) async-start(), calls=%async_computation.13 | async-start | bytes 4718592 | tf_op jit(solution)/shard_map/reduce_scatter | solution.py:38
  657.8 161.0 %all-reduce.32.cloned.1.call-start = ((), (), s32[]{:S(2)}) async-start(), calls=%async_computation.36 | async-start | bytes 1048576 | tf_op jit(solution)/shard_map/psum | solution.py:12
  721.3 325.4 %all-reduce.30.cloned.1.call-start = ((), (), s32[]{:S(2)}) async-start(), calls=%async_computation.35 | async-start | bytes 1048576 | tf_op jit(solution)/shard_map/psum | solution.py:12
  953.0 240.5 %all-gather.25.cloned.1.call-start = ((), (), s32[]{:S(2)}) async-start(), calls=%async_computation.24 | async-start | bytes 1310720 | tf_op jit(solution)/shard_map/all_gather | solution.py:36
  1110.6 41.3 %collective-permute-start.7 = (bf16[512,256]{0,1:T(8,128)(2,1)S(1)}, bf16[512,256]{0,1:T(8,128)(2,1)S(1)}, u32[]{:S(2)}, u32[]{:S(2)}) collective-permute-start(bf16[512,256]{0,1:T(8,128)(2,1)S(1)} %maximum_convert_fusion.4), channel_id=1, source_target_pairs={{0,0},{1,8},{2,16},{3,24},{4,1},{5,9},{6,17},{7,25},{8,2},{9,10},{... | collective-permute-start | bytes 786440 | tf_op jit(solution)/shard_map/ppermute | solution.py:35
  1152.0 0.7 copy-start.2
  1152.8 61.9 %all-gather.15.cloned.1.call-start = ((), (), s32[]{:S(2)}) async-start(), calls=%async_computation.14 | async-start | bytes 1310720 | tf_op jit(solution)/shard_map/all_gather | solution.py:36
  1178.1 14.5 collective-permute-start.2
  1192.6 0.7 copy-start.7
  1193.4 58.6 %reduce-scatter.25.cloned.1.call-start = ((), (), s32[]{:S(2)}) async-start(), calls=%async_computation.25 | async-start | bytes 4718592 | tf_op jit(solution)/shard_map/reduce_scatter | solution.py:38
  1206.1 82.3 %reduce-scatter.15.cloned.1.call-start = ((), (), s32[]{:S(2)}) async-start(), calls=%async_computation.15 | async-start | bytes 4718592 | tf_op jit(solution)/shard_map/reduce_scatter | solution.py:38
  1227.3 160.7 %all-reduce.28.cloned.1.call-start = ((), (), s32[]{:S(2)}) async-start(), calls=%async_computation.34 | async-start | bytes 1048576 | tf_op jit(solution)/shard_map/psum | solution.py:12
  1290.7 325.2 %all-reduce.26.cloned.1.call-start = ((), (), s32[]{:S(2)}) async-start(), calls=%async_computation.33 | async-start | bytes 1048576 | tf_op jit(solution)/shard_map/psum | solution.py:12
  1522.2 240.5 %all-gather.27.cloned.1.call-start = ((), (), s32[]{:S(2)}) async-start(), calls=%async_computation.26 | async-start | bytes 1310720 | tf_op jit(solution)/shard_map/all_gather | solution.py:36
  1679.9 41.3 %collective-permute-start.8 = (bf16[512,256]{0,1:T(8,128)(2,1)S(1)}, bf16[512,256]{0,1:T(8,128)(2,1)S(1)}, u32[]{:S(2)}, u32[]{:S(2)}) collective-permute-start(bf16[512,256]{0,1:T(8,128)(2,1)S(1)} %maximum_convert_fusion.5), channel_id=1, source_target_pairs={{0,0},{1,8},{2,16},{3,24},{4,1},{5,9},{6,17},{7,25},{8,2},{9,10},{... | collective-permute-start | bytes 786440 | tf_op jit(solution)/shard_map/ppermute | solution.py:35
  1721.2 0.7 copy-start.3
  1722.0 61.9 %all-gather.17.cloned.1.call-start = ((), (), s32[]{:S(2)}) async-start(), calls=%async_computation.16 | async-start | bytes 1310720 | tf_op jit(solution)/shard_map/all_gather | solution.py:36
  1747.3 14.5 collective-permute-start.3
  1761.8 0.7 copy-start.8
  1762.6 58.8 %reduce-scatter.27.cloned.1.call-start = ((), (), s32[]{:S(2)}) async-start(), calls=%async_computation.27 | async-start | bytes 4718592 | tf_op jit(solution)/shard_map/reduce_scatter | solution.py:38
  1775.3 82.7 %reduce-scatter.17.cloned.1.call-start = ((), (), s32[]{:S(2)}) async-start(), calls=%async_computation.17 | async-start | bytes 4718592 | tf_op jit(solution)/shard_map/reduce_scatter | solution.py:38
  1796.5 161.3 %all-reduce.24.cloned.1.call-start = ((), (), s32[]{:S(2)}) async-start(), calls=%async_computation.32 | async-start | bytes 1048576 | tf_op jit(solution)/shard_map/psum | solution.py:12
  1860.2 325.6 %all-reduce.22.cloned.1.call-start = ((), (), s32[]{:S(2)}) async-start(), calls=%async_computation.31 | async-start | bytes 1048576 | tf_op jit(solution)/shard_map/psum | solution.py:12
  2092.0 240.4 %all-gather.29.cloned.1.call-start = ((), (), s32[]{:S(2)}) async-start(), calls=%async_computation.28 | async-start | bytes 1310720 | tf_op jit(solution)/shard_map/all_gather | solution.py:36
  2249.7 41.3 %collective-permute-start.9 = (bf16[512,256]{0,1:T(8,128)(2,1)S(1)}, bf16[512,256]{0,1:T(8,128)(2,1)S(1)}, u32[]{:S(2)}, u32[]{:S(2)}) collective-permute-start(bf16[512,256]{0,1:T(8,128)(2,1)S(1)} %fusion.221), channel_id=1, source_target_pairs={{0,0},{1,8},{2,16},{3,24},{4,1},{5,9},{6,17},{7,25},{8,2},{9,10},{... | collective-permute-start | bytes 786440 | tf_op jit(solution)/shard_map/ppermute | solution.py:35
  2291.1 0.7 copy-start
  2291.8 61.8 %all-gather.19.cloned.1.call-start = ((), (), s32[]{:S(2)}) async-start(), calls=%async_computation.18 | async-start | bytes 1310720 | tf_op jit(solution)/shard_map/all_gather | solution.py:36
  2317.1 14.5 collective-permute-start.4
  2331.6 0.7 copy-start.9
  2332.4 58.6 %reduce-scatter.29.cloned.1.call-start = ((), (), s32[]{:S(2)}) async-start(), calls=%async_computation.29 | async-start | bytes 4718592 | tf_op jit(solution)/shard_map/reduce_scatter | solution.py:38
  2345.1 82.5 %reduce-scatter.19.cloned.1.call-start = ((), (), s32[]{:S(2)}) async-start(), calls=%async_computation.19 | async-start | bytes 4718592 | tf_op jit(solution)/shard_map/reduce_scatter | solution.py:38
  2366.3 161.1 %all-reduce.20.cloned.1.call-start = ((), (), s32[]{:S(2)}) async-start(), calls=%async_computation.30 | async-start | bytes 1048576 | tf_op jit(solution)/shard_map/psum | solution.py:12
Sparse Core Ops, SparseCore 0:
  25.5 27.2 all-gather.20
  54.9 21.2 all-gather.10
  78.5 35.1 reduce-scatter.20
  115.9 34.2 reduce-scatter.10
  153.9 95.8 all-reduce.35
  383.6 93.5 all-reduce.33
  583.4 21.2 all-gather.22
  624.0 21.1 all-gather.12
  647.5 35.1 reduce-scatter.22
  684.8 34.2 reduce-scatter.12
  722.9 95.8 all-reduce.31
  953.1 93.5 all-reduce.29
  1152.9 21.2 all-gather.24
  1193.5 21.1 all-gather.14
  1216.8 35.1 reduce-scatter.24
  1254.2 34.2 reduce-scatter.14
  1292.2 95.8 all-reduce.27
  1522.3 93.5 all-reduce.25
  1722.1 21.2 all-gather.26
  1762.7 21.1 all-gather.16
  1786.2 35.0 reduce-scatter.26
  1823.6 34.2 reduce-scatter.16
  1861.8 95.9 all-reduce.23
  2092.1 93.5 all-reduce.21
  2292.0 20.6 all-gather.28
  2332.5 21.1 all-gather.18
  2355.8 35.0 reduce-scatter.28
  2393.2 34.2 reduce-scatter.18
  2431.4 95.9 all-reduce.19
where the time goes:
time: 2550 us; the launch traced here: 2540 us
  waiting for transfers between devices  1280 us (50%)
  other arithmetic  906 us (36%)
  matrix products  201 us (8%)
  local copies, waits for them, and re-layouts  76.9 us (3%)
  starting transfers between devices  38.5 us (2%)
  between operations  37.1 us (1%)
    psum x9, waiting for transfers between devices, gram_total(): return lax.psum(local_gram, grid_axes)  860 us
    another operation x112, other arithmetic, cholqr_step(): chol_low = jnp.linalg.cholesky(gram_mat)  553 us
    another operation x35, other arithmetic, cholqr_step(): lax.linalg.triangular_solve(chol_low, y_mat, left_side=False, lower=True,...  318 us
    reduce_scatter x10, waiting for transfers between devices, apply_op(): lax.psum_scatter(partial_prod, 'col', scatter_dimension=0, tiled=True)  294 us
    dot_general x10, matrix products, apply_op(): partial_prod = jnp.dot(op_blk, x_col, preferred_element_type=jnp.float32)  126 us
    ppermute x10, waiting for transfers between devices, apply_op(): x_moved = lax.ppermute(x_sub.astype(jnp.bfloat16), grid_axes, perm_pairs)  68.1 us
    another operation x113, local copies, waits for them, and re-layouts, cholqr_step(): lax.linalg.triangular_solve(chol_low, y_mat, left_side=False, lower=True,...  63.8 us
    all_gather x10, waiting for transfers between devices, apply_op(): x_col = lax.all_gather(x_moved, 'row', axis=0, tiled=True)  52.8 us
  transfers between devices with their start and end apart: 39, of which 31 were waited for; matrix products, arithmetic and copies ran while one was open for 15% of the time, Pallas kernels for 0%

commit v1 on v0

v1 whole, which is shorter than its diff:
```python
import functools

import jax
import jax.numpy as jnp
from jax import lax
from jax.experimental import pallas as pl
from jax.experimental.pallas import tpu as pltpu
from jax.sharding import PartitionSpec as P

SWEEPS = 4
CORES = 2
RING = 4
PIVOTS = 32
GROUP = 8
VMEM_BYTES = 67043328
F32, BF16 = jnp.float32, jnp.bfloat16
TN = (((0,), (0,)), ((), ()))
NT = (((1,), (1,)), ((), ()))

AG_T, AG_A, RELAY, RS_T, RS_A, PAIR, GRAM_PAIR, GRAM_RS, GRAM_AG, LINV, MOVE = 0, 6, 12, 17, 23, 29, 33, 34, 35, 36, 37
COPIES = 40


def split3(v):
    high = v.astype(BF16)
    rest = v - high.astype(F32)
    mid = rest.astype(BF16)
    return high, mid, (rest - mid.astype(F32)).astype(BF16)


def dot_f32(lhs, rhs, dims):
    lh, lm, ll = split3(lhs)
    rh, rm, rl = split3(rhs)

    def one(a, b):
        return lax.dot_general(a, b, dims, preferred_element_type=F32)

    small = one(ll, rh) + one(lh, rl) + one(lm, rm)
    return (small + (one(lm, rh) + one(lh, rm))) + one(lh, rh)


def rows_of(ref, part, parts=2):
    size = ref.shape[0] // parts
    return ref.at[pl.ds(part * size, size)]


def inverse_factor(gram, work, store):
    tile = gram.shape[1]
    width = 2 * tile
    work[0:tile, 0:tile] = gram[0:tile]
    work[0:tile, tile:width] = gram[tile : 2 * tile]
    work[tile:width, tile:width] = gram[2 * tile : 3 * tile]
    at_row = lax.broadcasted_iota(jnp.int32, (width, width), 0)
    at_col = lax.broadcasted_iota(jnp.int32, (width, width), 1)
    work[:, width : 2 * width] = jnp.where(at_row == at_col, 1.0, 0.0).astype(F32)
    sub = lax.broadcasted_iota(jnp.int32, (GROUP, tile), 0)
    groups = PIVOTS // GROUP
    full = (GROUP, tile)

    def lane(row):
        return jnp.broadcast_to(row, full)

    for first in range(0, width, PIVOTS):
        near = first // tile
        offset = first - near * tile
        gram_tiles = list(range(near, 2))
        tiles = gram_tiles + [2 + i for i in range(near + 1)]
        data = {
            t: [work[pl.ds(first + GROUP * g, GROUP), t * tile : (t + 1) * tile] for g in range(groups)] for t in tiles
        }
        cols = [
            {g: jnp.broadcast_to(data[near][g][:, offset + j : offset + j + 1], full) for g in range(j // GROUP, groups)}
            for j in range(PIVOTS)
        ]
        pivots = [jnp.ones(full, F32) for _ in range(groups)]
        for j in range(PIVOTS):
            gj, rj = divmod(j, GROUP)
            col = cols[j]
            pivot = lane(col[gj][rj : rj + 1])
            inv = 1.0 / pivot
            pivots[gj] = jnp.where(sub == rj, pivot, pivots[gj])
            for nxt in range(j + 1, PIVOTS):
                gn, rn = divmod(nxt, GROUP)
                entry = lane(col[gn][rn : rn + 1])
                if nxt == j + 1:
                    for g in range(gn, groups):
                        cols[nxt][g] = cols[nxt][g] - (col[g] * entry) * inv
                else:
                    scaled = entry * inv
                    for g in range(gn, groups):
                        cols[nxt][g] = cols[nxt][g] - col[g] * scaled
            for g in range(gj, groups):
                factor = col[g] * inv
                if g == gj:
                    if rj == GROUP - 1:
                        continue
                    factor = jnp.where(sub > rj, factor, 0.0)
                for t in tiles:
                    data[t][g] = data[t][g] - factor * lane(data[t][gj][rj : rj + 1])
        scale = [lax.rsqrt(p) for p in pivots]
        for t in tiles:
            data[t] = [d * s for d, s in zip(data[t], scale, strict=True)]
        for t in tiles:
            if t >= 2:
                for g in range(groups):
                    store(first + GROUP * g, t - 2, data[t][g])
        nxt = first + PIVOTS
        if nxt == width:
            break
        parts = {t: split3(jnp.concatenate(data[t], axis=0)) for t in tiles}
        below = [t for t in gram_tiles if (t + 1) * tile > nxt]
        low = below[0] * tile
        order_l, order_r = (0, 0, 1, 0, 2, 1), (0, 1, 0, 2, 0, 1)
        lhs = jnp.concatenate([jnp.concatenate([parts[t][i] for i in order_l], axis=0) for t in below], axis=1)
        right_tiles = below + [t for t in tiles if t >= 2]
        rhs = jnp.concatenate([jnp.concatenate([parts[t][i] for i in order_r], axis=0) for t in right_tiles], axis=1)
        upd = lax.dot_general(lhs, rhs, TN, preferred_element_type=F32)
        for n, t in enumerate(right_tiles):
            where = pl.ds(nxt, width - nxt), slice(t * tile, (t + 1) * tile)
            work[where] = work[where] - upd[nxt - low :, n * tile : (n + 1) * tile]


def kernel(
    sizes, left_op, left_start, right_op, right_start, left_out, left_ray, right_out, right_ray,
    ops, ycur, ag_t, ag_a, p_t, p_a, d_a, r_t, r_a, x_half, x_move, g_loc, g_pair, g_sum, g_in, g_all, h_all, work, linv,
    send, recv, load_sem,
):
    nrow, ncol, total_rows = sizes
    sub, width = ycur.shape[1:]
    tile = width // 2
    nchips = RING * RING
    y = lax.axis_index("row")
    c = lax.axis_index("col")
    x, k = lax.div(c, CORES), lax.rem(c, CORES)
    other = 1 - k
    xp, xm, xf = (lax.rem(x + d, RING) for d in (1, 3, 2))
    yp, ym, yf = (lax.rem(y + d, RING) for d in (1, 3, 2))

    def dev(row, chip, core):
        return {"row": row, "col": chip * CORES + core}

    partner = dev(y, x, other)

    def push(i, src, dst, to):
        return pltpu.make_async_remote_copy(
            src_ref=src, dst_ref=dst, send_sem=send.at[i], recv_sem=recv.at[i], device_id=to, device_id_type=pl.DeviceIdType.MESH
        )

    loads = []
    for n, (xi, yi) in enumerate(((x, y), (xm, ym), (xp, yp), (xf, yf))):
        take = pl.ds(pl.multiple_of(xi * CORES * sub, sub), CORES * sub)
        loads.append(pltpu.make_async_copy(left_op.at[take], ops.at[0, take], load_sem.at[2 * n]))
        take = pl.ds(pl.multiple_of(yi * sub, sub), sub)
        loads.append(pltpu.make_async_copy(right_op.at[:, take], ops.at[1, :, take], load_sem.at[2 * n + 1]))
    starts = [
        pltpu.make_async_copy(left_start, ycur.at[0], load_sem.at[8]),
        pltpu.make_async_copy(right_start, ycur.at[1], load_sem.at[9]),
    ]
    for copy in starts + loads:
        copy.start()

    barrier = pltpu.get_barrier_semaphore()
    here = y * ncol + c
    for o in range(1, nrow * ncol):
        there = lax.rem(here + o, nrow * ncol)
        pl.semaphore_signal(
            barrier, inc=1, device_id={"row": lax.div(there, ncol), "col": lax.rem(there, ncol)}, device_id_type=pl.DeviceIdType.MESH
        )
    pl.semaphore_wait(barrier, nrow * ncol - 1)

    by_row, by_col = y * ncol + c, c * nrow + y
    to_col_y, to_col_c = lax.rem(by_row, nrow), lax.div(by_row, nrow)
    to_row_y, to_row_c = lax.div(by_col, ncol), lax.rem(by_col, ncol)
    stays = by_row == by_col

    for copy in starts:
        copy.wait()
    ag_t[c] = ycur[0].T.astype(BF16)
    x_half[...] = ycur[1].astype(BF16)
    first_move = push(MOVE, x_half, ag_a.at[to_col_y], {"row": to_col_y, "col": to_col_c})

    @pl.when(stays)
    def _():
        ag_a[y] = x_half[...]

    @pl.when(jnp.logical_not(stays))
    def _():
        first_move.start()
        first_move.wait()

    def ring_gather(base, blk, me, plus, minus, far, to):
        own = [rows_of(blk(me), h) for h in range(2)]
        first = [
            push(base + 0, own[0], own[0], to(plus)),
            push(base + 1, own[1], own[1], to(plus)),
            push(base + 2, own[1], own[1], to(minus)),
            push(base + 3, own[0], own[0], to(minus)),
        ]
        got0, got1 = rows_of(blk(minus), 0), rows_of(blk(plus), 1)
        return first, [push(base + 4, got0, got0, to(plus)), push(base + 5, got1, got1, to(minus))]

    def apply(p):
        t = lax.rem(p, 2)
        a = 1 - t

        def mm_t(chip, owner, first):
            lanes = pl.ds(pl.multiple_of(owner * sub, sub), sub)
            acc = None
            for core in range(CORES):
                b = chip * CORES + core
                rows = pl.ds(pl.multiple_of(b * sub, sub), sub)
                one = jnp.dot(ag_t[b], ops[t, rows, lanes], preferred_element_type=F32)
                acc = one if acc is None else acc + one
            p_t[owner] = acc if first else p_t[owner] + acc

        def mm_a(chip, owner, first):
            rows = pl.ds(pl.multiple_of(owner * sub, sub), sub)
            lanes = pl.ds(pl.multiple_of(chip * sub, sub), sub)
            acc = jnp.dot(ops[a, rows, lanes], ag_a[chip], preferred_element_type=F32)
            p_a[owner] = acc if first else p_a[owner] + acc

        def loaded(n):
            @pl.when(p == 0)
            def _():
                loads[n].wait()

        send_t, fwd_t = ring_gather(AG_T, lambda i: ag_t.at[i * CORES + k], x, xp, xm, xf, lambda i: dev(y, i, k))
        send_a, fwd_a = ring_gather(AG_A, lambda i: ag_a.at[i], y, yp, ym, yf, lambda i: dev(i, x, k))

        def relay(n, i, h=None):
            ref = ag_t.at[i * CORES + k]
            ref = ref if h is None else rows_of(ref, h)
            return push(RELAY + n, ref, ref, partner)

        relays = [relay(0, x), relay(1, xm), relay(2, xp), relay(3, xf, 0), relay(4, xf, 1)]
        for n in (0, 2, 1, 3):
            send_t[n].start()
            send_a[n].start()
        relays[0].start()
        loaded(1)
        for owner in range(RING * CORES):
            mm_a(y, owner, True)
        relays[0].wait_recv()
        loaded(0)
        for owner in range(RING):
            mm_t(x, owner, True)
        send_t[0].wait_recv()
        fwd_t[0].start()
        send_a[0].wait_recv()
        fwd_a[0].start()
        send_t[2].wait_recv()
        fwd_t[1].start()
        send_a[2].wait_recv()
        fwd_a[1].start()
        send_t[1].wait_recv()
        relays[1].start()
        send_t[3].wait_recv()
        relays[2].start()
        send_a[1].wait_recv()
        loaded(3)
        for owner in range(RING * CORES):
            mm_a(ym, owner, False)
        send_a[3].wait_recv()
        loaded(5)
        for owner in range(RING * CORES):
            mm_a(yp, owner, False)
        relays[1].wait_recv()
        loaded(2)
        for owner in range(RING):
            mm_t(xm, owner, False)
        relays[2].wait_recv()
        loaded(4)
        for owner in range(RING):
            mm_t(xp, owner, False)
        fwd_t[0].wait_recv()
        relays[3].start()
        fwd_t[1].wait_recv()
        relays[4].start()
        fwd_a[0].wait_recv()
        fwd_a[1].wait_recv()

        loaded(7)
        pairs = []
        for n, i in enumerate((xf, xp, xm, x)):
            mm_a(yf, i * CORES + other, False)
            pairs.append(push(PAIR + n, p_a.at[i * CORES + other], d_a.at[i], partner))
            pairs[n].start()

        def ring_scatter(base, part, got, plus, minus, far, to):
            def half(i, h):
                return rows_of(part(i), h)

            return [
                push(base + 0, half(far, 0), got.at[0], to(plus)),
                push(base + 1, half(far, 1), got.at[1], to(minus)),
                push(base + 2, half(plus, 1), got.at[2], to(plus)),
                push(base + 3, half(minus, 0), got.at[3], to(minus)),
                push(base + 4, half(plus, 0), got.at[4], to(plus)),
                push(base + 5, half(minus, 1), got.at[5], to(minus)),
            ]

        out_t = ring_scatter(RS_T, lambda i: p_t.at[i], r_t, yp, ym, yf, lambda i: dev(i, x, k))
        out_a = ring_scatter(RS_A, lambda i: p_a.at[i * CORES + k], r_a, xp, xm, xf, lambda i: dev(y, i, k))
        relays[3].wait_recv()
        relays[4].wait_recv()
        loaded(6)
        for n, i in enumerate((yf, yp, ym, y)):
            mm_t(xf, i, False)
            for q in ((0, 1), (2,), (3,), ())[n]:
                out_t[q].start()
        for n, i in enumerate((xf, xp, xm, x)):
            mm_a(yf, i * CORES + k, False)
            pairs[n].wait_recv()
            p_a[i * CORES + k] = p_a[i * CORES + k] + d_a[i]
            for q in ((0, 1), (2,), (3,), ())[n]:
                out_a[q].start()
        ht, ha = width // 2, sub // 2
        out_t[0].wait_recv()
        p_t[yp, 0:ht] = p_t[yp, 0:ht] + r_t[0]
        out_t[4].start()
        out_t[1].wait_recv()
        p_t[ym, ht:width] = p_t[ym, ht:width] + r_t[1]
        out_t[5].start()
        out_a[0].wait_recv()
        kp, km, kk = xp * CORES + k, xm * CORES + k, x * CORES + k
        p_a[kp, 0:ha] = p_a[kp, 0:ha] + r_a[0]
        out_a[4].start()
        out_a[1].wait_recv()
        p_a[km, ha:sub] = p_a[km, ha:sub] + r_a[1]
        out_a[5].start()
        for n in (2, 3, 4, 5):
            out_t[n].wait_recv()
            out_a[n].wait_recv()
        ycur[t, :, 0:ht] = (p_t[y, 0:ht] + r_t[3] + r_t[4]).T
        ycur[t, :, ht:width] = (p_t[y, ht:width] + r_t[2] + r_t[5]).T
        ycur[a, 0:ha] = p_a[kk, 0:ha] + r_a[3] + r_a[4]
        ycur[a, ha:sub] = p_a[kk, ha:sub] + r_a[2] + r_a[5]
        for copy in send_t + fwd_t + send_a + fwd_a + relays + pairs + out_t + out_a:
            copy.wait_send()

    def all_reduce(rows):
        piece = rows // nchips
        pair = push(GRAM_PAIR, g_loc.at[other, pl.ds(0, rows)], g_pair.at[pl.ds(0, rows)], partner)
        pair.start()
        pair.wait_recv()
        g_sum[0:rows] = g_loc[k, 0:rows] + g_pair[0:rows]

        def chunk(ref, q):
            return ref.at[pl.ds(pl.multiple_of(q * piece, GROUP), piece)]

        def chips():
            for o in range(1, nchips):
                to_y, to_x = lax.rem(y + o // RING, RING), lax.rem(x + o % RING, RING)
                yield o, to_y * RING + to_x, dev(to_y, to_x, k)

        mine = y * RING + x
        for o, q, to in chips():
            push(GRAM_RS, chunk(g_sum, q), chunk(g_in, o - 1), to).start()
        others = pl.ds(0, (nchips - 1) * piece)
        pltpu.make_async_copy(g_in.at[others], g_in.at[others], recv.at[GRAM_RS]).wait()
        total = chunk(g_sum, mine)[...]
        for o in range(1, nchips):
            total = total + g_in[(o - 1) * piece : o * piece]
        chunk(g_all, mine)[...] = total / total_rows
        for o, q, to in chips():
            push(GRAM_AG, chunk(g_all, mine), chunk(g_all, mine), to).start()
        pltpu.make_async_copy(g_in.at[others], g_in.at[others], recv.at[GRAM_AG]).wait()
        pair.wait_send()
        for i in (GRAM_RS, GRAM_AG):
            pltpu.make_async_copy(g_in.at[others], g_in.at[others], send.at[i]).wait()

    def gram_blocks(op, dot):
        lo, hi = ycur[op, :, 0:tile], ycur[op, :, tile:width]
        g_loc[op, 0:tile] = dot(lo, lo)
        g_loc[op, tile : 2 * tile] = dot(lo, hi)
        g_loc[op, 2 * tile : 3 * tile] = dot(hi, hi)

    def half_dot(u, v):
        return lax.dot_general(u.astype(BF16), v.astype(BF16), TN, preferred_element_type=F32)

    def full_dot(u, v):
        return dot_f32(u, v, TN)

    def normalize(q):
        @pl.when(q == 0)
        def _():
            for op in range(2):
                gram_blocks(op, half_dot)

        @pl.when(q == 1)
        def _():
            for op in range(2):
                gram_blocks(op, full_dot)

        all_reduce(3 * tile)

        def store(first, t, value):
            linv[k, pl.ds(first, GROUP), t * tile : (t + 1) * tile] = value

        linv[k, 0:tile, tile:width] = jnp.zeros((tile, tile), F32)
        inverse_factor(g_all, work, store)
        swap = push(LINV, linv.at[k], linv.at[k], partner)
        swap.start()
        ycur[k] = dot_f32(ycur[k], linv[k], NT)
        swap.wait_recv()
        ycur[other] = dot_f32(ycur[other], linv[other], NT)
        swap.wait_send()

    keep_left = push(MOVE + 1, ycur.at[0], x_move.at[0], {"row": to_col_y, "col": to_col_c})
    keep_right = push(MOVE + 2, ycur.at[1], x_move.at[1], {"row": to_row_y, "col": to_row_c})

    def sweep(p, carry):
        apply(p)

        @pl.when(p < SWEEPS)
        def _():
            def one(q, carry):
                normalize(q)
                return carry

            lax.fori_loop(0, 2, one, 0)
            nxt = lax.rem(p + 1, 2)
            ag_t[c] = ycur[nxt].T.astype(BF16)
            ag_a[y] = ycur[1 - nxt].astype(BF16)

        @pl.when(p == SWEEPS - 1)
        def _():
            left_out[...] = ycur[0]

            @pl.when(stays)
            def _():
                x_move[...] = ycur[...]

            @pl.when(jnp.logical_not(stays))
            def _():
                keep_left.start()
                keep_right.start()
                keep_left.wait()
                keep_right.wait()

        return carry

    lax.fori_loop(0, SWEEPS + 1, sweep, 0)
    right_out[...] = x_move[1]
    for op in range(2):
        for n, (i, j) in enumerate(((0, 0), (0, 1), (1, 0), (1, 1))):
            xs, zs = slice(i * tile, (i + 1) * tile), slice(j * tile, (j + 1) * tile)
            g_loc[op, n * tile : (n + 1) * tile] = dot_f32(x_move[op, :, xs], ycur[op, :, zs], TN)
    all_reduce(4 * tile)
    swap = push(LINV, g_all, h_all, partner)
    swap.start()
    swap.wait()
    for n, (i, j) in enumerate(((0, 0), (0, 1), (1, 0), (1, 1))):
        rows, at = slice(n * tile, (n + 1) * tile), (slice(i * tile, (i + 1) * tile), slice(j * tile, (j + 1) * tile))
        left_ray[at] = jnp.where(k == 0, g_all[rows], h_all[rows])
        right_ray[at] = jnp.where(k == 0, h_all[rows], g_all[rows])


def solution(mesh):
    nrow, ncol = mesh.shape["row"], mesh.shape["col"]
    assert nrow == RING and ncol == RING * CORES

    def local_program(left_op, left_start, right_op, right_start):
        rows, cols = left_op.shape
        sub, width = left_start.shape
        tile = width // 2
        vmem = pltpu.VMEM
        dma = pltpu.SemaphoreType.DMA
        out = [
            jax.ShapeDtypeStruct((sub, width), F32),
            jax.ShapeDtypeStruct((width, width), F32),
        ] * 2
        return pl.pallas_call(
            functools.partial(kernel, (nrow, ncol, rows * nrow)),
            out_shape=out,
            in_specs=[pl.BlockSpec(memory_space=pl.ANY)] * 4,
            out_specs=[pl.BlockSpec(memory_space=vmem)] * 4,
            scratch_shapes=[
                vmem((2, rows, cols), BF16),
                vmem((2, sub, width), F32),
                vmem((ncol, width, sub), BF16),
                vmem((nrow, sub, width), BF16),
                vmem((nrow, width, sub), F32),
                vmem((ncol, sub, width), F32),
                vmem((RING, sub, width), F32),
                vmem((6, width // 2, sub), F32),
                vmem((6, sub // 2, width), F32),
                vmem((sub, width), BF16),
                vmem((2, sub, width), F32),
                vmem((2, 4 * tile, tile), F32),
                vmem((4 * tile, tile), F32),
                vmem((4 * tile, tile), F32),
                vmem((4 * tile, tile), F32),
                vmem((4 * tile, tile), F32),
                vmem((4 * tile, tile), F32),
                vmem((width, 2 * width), F32),
                vmem((2, width, width), F32),
                dma((COPIES,)),
                dma((COPIES,)),
                dma((10,)),
            ],
            compiler_params=pltpu.CompilerParams(collective_id=0, has_side_effects=True, vmem_limit_bytes=VMEM_BYTES),
            name="subspace",
        )(left_op, left_start, right_op, right_start)

    op_spec = P(("batch", "row"), "col")
    vec_spec = P(("batch", "row", "col"), None)
    small_spec = P("batch", None)
    return jax.shard_map(
        local_program,
        mesh=mesh,
        in_specs=(op_spec, vec_spec, op_spec, vec_spec),
        out_specs=(vec_spec, small_spec, vec_spec, small_spec),
        check_vma=False,
    )
```

time: 2550 us -> 447 us (0.18)
  waiting for transfers between devices: 1280 us -> 0 us
  other arithmetic: 906 us -> 0 us
  Pallas kernels: 0 us -> 439 us
  matrix products: 201 us -> 0 us
  local copies, waits for them, and re-layouts: 76.9 us -> 7.07 us
  starting transfers between devices: 38.5 us -> 0 us
  between operations: 37.1 us -> 0.64 us
    another operation x147 -> x0, other arithmetic: 871 us -> none  [the longest x112 553 us: cholqr_step(): chol_low = jnp.linalg.cholesky(gram_mat)]
    psum x9 -> x0, waiting for transfers between devices: 860 us -> none  [gram_total(): return lax.psum(local_gram, grid_axes)]
    pallas_call x0 -> x1, Pallas kernels: none -> 439 us  [local_program(): pl.pallas_call(functools.partial(kernel, (nrow, ncol, rows * nrow)), out_...]
    reduce_scatter x10 -> x0, waiting for transfers between devices: 294 us -> none  [apply_op(): lax.psum_scatter(partial_prod, 'col', scatter_dimension=0, tiled=True)]
    dot_general x28 -> x0, matrix products: 158 us -> none  [the longest x10 126 us: apply_op(): partial_prod = jnp.dot(op_blk, x_col, preferred_element_type=jnp.float32)]
    ppermute x10 -> x0, waiting for transfers between devices: 68.1 us -> none  [apply_op(): x_moved = lax.ppermute(x_sub.astype(jnp.bfloat16), grid_axes, perm_pairs)]
    another operation x145 -> x0, local copies, waits for them, and re-layouts: 64.2 us -> none  [the longest x113 63.8 us: cholqr_step(): lax.linalg.triangular_solve(chol_low, y_mat, left_side=False, lower=True,...]
    all_gather x10 -> x0, waiting for transfers between devices: 52.8 us -> none  [apply_op(): x_col = lax.all_gather(x_moved, 'row', axis=0, tiled=True)]
  transfers between devices with their start and end apart: 39 -> 0, of which waited for: 31 -> 0; matrix products, arithmetic and copies ran while one was open for 15% -> 0% of each run, Pallas kernels for 0% -> 0%
where the time goes in v1:
time: 447 us; the launch traced here: 446 us
  Pallas kernels  439 us (98%)
  local copies, waits for them, and re-layouts  7.07 us (2%)
    pallas_call x1, Pallas kernels, local_program(): pl.pallas_call(functools.partial(kernel, (nrow, ncol, rows * nrow)), out_...  439 us

profile of v1, /device:TPU:97, one launch (start us, length us, event | category | flops | bytes accessed | tf_op | source)
XLA Modules:
  0.0 446.4 jit_solution(6111307676344536477)
XLA Ops:
  0.6 438.7 %subspace.1 = (f32[512,256]{1,0:T(8,128)}, f32[256,256]{1,0:T(8,128)}, f32[512,256]{1,0:T(8,128)}, f32[256,256]{1,0:T(8,128)}) custom-call(bf16[4096,2048]{1,0:T(8,128)(2,1)} %left_op.1, f32[512,256]{1,0:T(8,128)} %left_start.1, bf16[4096,2048]{1,0:T(8,128)(2,1)} %right_op.1, f32[512,256]{1,0:T(8,128)} %right_start.1), custom_call_target="tpu_custom_call" | custom-call | tf_op jit(solution)/shard_map/subspace/pallas_call | solution.py:473
  439.4 1.9 copy.12
  441.2 1.7 copy.13
  442.9 1.9 copy.14
  444.8 1.7 copy.15

commit v2 on v1

v2 whole, which is shorter than its diff:
```python
import functools

import jax
import jax.numpy as jnp
from jax import lax
from jax.experimental import pallas as pl
from jax.experimental.pallas import tpu as pltpu
from jax.sharding import PartitionSpec as P

SWEEPS = 4
CORES = 2
RING = 4
PIVOTS = 32
GROUP = 8
VMEM_BYTES = 67043328
F32, BF16 = jnp.float32, jnp.bfloat16
TN = (((0,), (0,)), ((), ()))
NT = (((1,), (1,)), ((), ()))

AG_T, AG_A, RELAY, RS_T, RS_A, PAIR, GRAM_PAIR, GRAM_RS, GRAM_AG, LINV, MOVE = 0, 6, 12, 19, 25, 31, 35, 36, 37, 38, 39
COPIES = 42


def split3(v):
    high = v.astype(BF16)
    rest = v - high.astype(F32)
    mid = rest.astype(BF16)
    return high, mid, (rest - mid.astype(F32)).astype(BF16)


def dot_f32(lhs, rhs, dims):
    lh, lm, ll = split3(lhs)
    rh, rm, rl = split3(rhs)

    def one(a, b):
        return lax.dot_general(a, b, dims, preferred_element_type=F32)

    small = one(ll, rh) + one(lh, rl) + one(lm, rm)
    return (small + (one(lm, rh) + one(lh, rm))) + one(lh, rh)


class Phases:
    def __init__(self):
        self.scope = None

    def __call__(self, name=None):
        if self.scope is not None:
            self.scope.__exit__(None, None, None)
        self.scope = None
        if name is not None:
            self.scope = jax.named_scope(name)
            self.scope.__enter__()


def rows_of(ref, part, parts=2):
    size = ref.shape[0] // parts
    return ref.at[pl.ds(part * size, size)]


def inverse_factor(gram, work, store):
    tile = gram.shape[1]
    width = 2 * tile
    work[0:tile, 0:tile] = gram[0:tile]
    work[0:tile, tile:width] = gram[tile : 2 * tile]
    work[tile:width, tile:width] = gram[2 * tile : 3 * tile]
    at_row = lax.broadcasted_iota(jnp.int32, (width, width), 0)
    at_col = lax.broadcasted_iota(jnp.int32, (width, width), 1)
    work[:, width : 2 * width] = jnp.where(at_row == at_col, 1.0, 0.0).astype(F32)
    sub = lax.broadcasted_iota(jnp.int32, (GROUP, tile), 0)
    groups = PIVOTS // GROUP
    full = (GROUP, tile)

    def lane(row):
        return jnp.broadcast_to(row, full)

    for first in range(0, width, PIVOTS):
        near = first // tile
        offset = first - near * tile
        gram_tiles = list(range(near, 2))
        tiles = gram_tiles + [2 + i for i in range(near + 1)]
        data = {
            t: [work[pl.ds(first + GROUP * g, GROUP), t * tile : (t + 1) * tile] for g in range(groups)] for t in tiles
        }
        cols = [
            {g: jnp.broadcast_to(data[near][g][:, offset + j : offset + j + 1], full) for g in range(j // GROUP, groups)}
            for j in range(PIVOTS)
        ]
        pivots = [jnp.ones(full, F32) for _ in range(groups)]
        for j in range(PIVOTS):
            gj, rj = divmod(j, GROUP)
            col = cols[j]
            pivot = lane(col[gj][rj : rj + 1])
            inv = 1.0 / pivot
            pivots[gj] = jnp.where(sub == rj, pivot, pivots[gj])
            for nxt in range(j + 1, PIVOTS):
                gn, rn = divmod(nxt, GROUP)
                entry = lane(col[gn][rn : rn + 1])
                if nxt == j + 1:
                    for g in range(gn, groups):
                        cols[nxt][g] = cols[nxt][g] - (col[g] * entry) * inv
                else:
                    scaled = entry * inv
                    for g in range(gn, groups):
                        cols[nxt][g] = cols[nxt][g] - col[g] * scaled
            for g in range(gj, groups):
                factor = col[g] * inv
                if g == gj:
                    if rj == GROUP - 1:
                        continue
                    factor = jnp.where(sub > rj, factor, 0.0)
                for t in tiles:
                    data[t][g] = data[t][g] - factor * lane(data[t][gj][rj : rj + 1])
        scale = [lax.rsqrt(p) for p in pivots]
        for t in tiles:
            data[t] = [d * s for d, s in zip(data[t], scale, strict=True)]
        for t in tiles:
            if t >= 2:
                for g in range(groups):
                    store(first + GROUP * g, t - 2, data[t][g])
        nxt = first + PIVOTS
        if nxt == width:
            break
        parts = {t: split3(jnp.concatenate(data[t], axis=0)) for t in tiles}
        below = [t for t in gram_tiles if (t + 1) * tile > nxt]
        low = below[0] * tile
        order_l, order_r = (0, 0, 1, 0, 2, 1), (0, 1, 0, 2, 0, 1)
        lhs = jnp.concatenate([jnp.concatenate([parts[t][i] for i in order_l], axis=0) for t in below], axis=1)
        right_tiles = below + [t for t in tiles if t >= 2]
        rhs = jnp.concatenate([jnp.concatenate([parts[t][i] for i in order_r], axis=0) for t in right_tiles], axis=1)
        upd = lax.dot_general(lhs, rhs, TN, preferred_element_type=F32)
        for n, t in enumerate(right_tiles):
            where = pl.ds(nxt, width - nxt), slice(t * tile, (t + 1) * tile)
            work[where] = work[where] - upd[nxt - low :, n * tile : (n + 1) * tile]


def kernel(
    sizes, left_op, left_start, right_op, right_start, x_out, h_out,
    ops, ycur, ag_t, ag_a, p_t, p_a, d_a, r_t, r_a, x_half, y_keep, x_move, g_loc, g_pair, g_sum, g_in, g_all, h_all, work, linv,
    send, recv, load_sem,
):
    nrow, ncol, total_rows = sizes
    sub, width = ycur.shape[1:]
    tile, hsub = width // 2, sub // 2
    nchips = RING * RING
    y = lax.axis_index("row")
    c = lax.axis_index("col")
    x, k = lax.div(c, CORES), lax.rem(c, CORES)
    other = 1 - k
    xp, xm, xf = (lax.rem(x + d, RING) for d in (1, 3, 2))
    yp, ym, yf = (lax.rem(y + d, RING) for d in (1, 3, 2))

    def dev(row, chip, core):
        return {"row": row, "col": chip * CORES + core}

    partner = dev(y, x, other)

    def push(i, src, dst, to):
        return pltpu.make_async_remote_copy(
            src_ref=src, dst_ref=dst, send_sem=send.at[i], recv_sem=recv.at[i], device_id=to, device_id_type=pl.DeviceIdType.MESH
        )

    def spot(i):
        return lax.rem(i + RING - x, RING)

    def run(index, size):
        return pl.ds(pl.multiple_of(index * size, size), size)

    phase = Phases()
    phase("boot")
    starts = [
        pltpu.make_async_copy(left_start, ycur.at[0], load_sem.at[8]),
        pltpu.make_async_copy(right_start, ycur.at[1], load_sem.at[9]),
    ]
    loads_t, loads_a = [], []
    for n, (xi, yi) in enumerate(((x, y), (xm, ym), (xp, yp), (xf, yf))):
        take = run(xi, CORES * sub)
        loads_t.append(pltpu.make_async_copy(left_op.at[take], ops.at[0, take], load_sem.at[2 * n]))
        take = run(spot(yi), sub)
        loads_a.append(pltpu.make_async_copy(right_op.at[:, take], ops.at[1, :, take], load_sem.at[2 * n + 1]))
    for copy in starts + loads_t + loads_a:
        copy.start()

    barrier = pltpu.get_barrier_semaphore()
    here = y * ncol + c
    for o in range(1, nrow * ncol):
        there = lax.rem(here + o, nrow * ncol)
        pl.semaphore_signal(
            barrier, inc=1, device_id={"row": lax.div(there, ncol), "col": lax.rem(there, ncol)}, device_id_type=pl.DeviceIdType.MESH
        )

    in_col = lax.rem(c, nrow)
    to_col_c = y * CORES + lax.div(c, nrow)
    to_col_y = lax.rem(y + in_col, RING)
    to_row_y = x
    to_row_c = k * nrow + spot(y)
    stays = jnp.logical_and(to_col_c == c, to_col_y == y)
    leaves = jnp.logical_not(stays)

    for copy in starts:
        copy.wait()
    for h in range(2):
        ag_t[c, h] = ycur[0, h * hsub : (h + 1) * hsub].T.astype(BF16)
    x_half[...] = ycur[1].astype(BF16)
    pl.semaphore_wait(barrier, nrow * ncol - 1)
    first_moves = [
        push(MOVE + h, x_half.at[pl.ds(h * hsub, hsub)], ag_a.at[to_col_y, h], {"row": to_col_y, "col": to_col_c}) for h in range(2)
    ]

    @pl.when(leaves)
    def _():
        for copy in first_moves:
            copy.start()

    phase()

    def ring_gather(base, blk, me, plus, minus, to):
        own = [blk(me, h) for h in range(2)]
        first = [
            push(base + 0, own[0], own[0], to(plus)),
            push(base + 1, own[1], own[1], to(plus)),
            push(base + 2, own[1], own[1], to(minus)),
            push(base + 3, own[0], own[0], to(minus)),
        ]
        got0, got1 = blk(minus, 0), blk(plus, 1)
        return first, [push(base + 4, got0, got0, to(plus)), push(base + 5, got1, got1, to(minus))]

    def ring_scatter(base, part, got, plus, minus, far, to):
        def half(i, h):
            return rows_of(part(i), h)

        return [
            push(base + 0, half(far, 0), got.at[0], to(plus)),
            push(base + 1, half(far, 1), got.at[1], to(minus)),
            push(base + 2, half(plus, 1), got.at[2], to(plus)),
            push(base + 3, half(minus, 0), got.at[3], to(minus)),
            push(base + 4, half(plus, 0), got.at[4], to(plus)),
            push(base + 5, half(minus, 1), got.at[5], to(minus)),
        ]

    keep_left = push(MOVE, y_keep.at[0], x_move.at[0], {"row": to_col_y, "col": to_col_c})
    keep_right = push(MOVE + 1, y_keep.at[1], x_move.at[1], {"row": to_row_y, "col": to_row_c})
    out_left = pltpu.make_async_copy(y_keep.at[0], x_out.at[0], load_sem.at[0])
    out_right = pltpu.make_async_copy(x_move.at[1], x_out.at[1], load_sem.at[1])

    def apply(p):
        t = lax.rem(p, 2)
        a = 1 - t

        def mm_t(pieces, owner, first=False):
            acc = None
            for chip, h in pieces:
                for core in range(CORES):
                    b = chip * CORES + core
                    one = jnp.dot(ag_t[b, h], ops[t, run(b * 2 + h, hsub), run(spot(owner), sub)], preferred_element_type=F32)
                    acc = one if acc is None else acc + one
            p_t[owner] = acc if first else p_t[owner] + acc

        def mm_a(pieces, owner, first=False):
            acc = None
            for i, h in pieces:
                one = jnp.dot(ops[a, run(owner, sub), run(spot(i) * 2 + h, hsub)], ag_a[i, h], preferred_element_type=F32)
                acc = one if acc is None else acc + one
            p_a[owner] = acc if first else p_a[owner] + acc

        def loaded(copy):
            @pl.when(p == 0)
            def _():
                copy.wait()

        send_t, fwd_t = ring_gather(AG_T, lambda i, h: ag_t.at[i * CORES + k, h], x, xp, xm, lambda i: dev(y, i, k))
        send_a, fwd_a = ring_gather(AG_A, lambda i, h: ag_a.at[i, h], y, yp, ym, lambda i: dev(i, x, k))

        def relay(n, i, h=None):
            ref = ag_t.at[i * CORES + k] if h is None else ag_t.at[i * CORES + k, h]
            return push(RELAY + n, ref, ref, partner)

        relays = [relay(0, x)] + [relay(1 + n, i, h) for n, (i, h) in enumerate(((xm, 0), (xp, 1), (xm, 1), (xp, 0), (xf, 0), (xf, 1)))]
        own_y = [(y, 0), (y, 1)]
        phase("ag_own")
        for n in (0, 2, 1, 3):
            send_t[n].start()
        relays[0].start()

        @pl.when(p > 0)
        def _():
            for n in (0, 2, 1, 3):
                send_a[n].start()
            for owner in range(RING * CORES):
                mm_a(own_y, owner, True)

        relays[0].wait_recv()
        loaded(loads_t[0])
        for owner in range(RING):
            mm_t([(x, 0), (x, 1)], owner, True)

        @pl.when(p == 0)
        def _():
            @pl.when(leaves)
            def _():
                for copy in first_moves:
                    copy.wait()

            @pl.when(stays)
            def _():
                for h in range(2):
                    ag_a[y, h] = x_half[h * hsub : (h + 1) * hsub]

            for n in (0, 2, 1, 3):
                send_a[n].start()
            loads_a[0].wait()
            for owner in range(RING * CORES):
                mm_a(own_y, owner, True)

        phase("ag_wait1")
        for n, fwd in ((0, 0), (2, 1)):
            send_t[n].wait_recv()
            fwd_t[fwd].start()
            relays[1 + fwd].start()
        for n, fwd in ((0, 0), (2, 1)):
            send_a[n].wait_recv()
            fwd_a[fwd].start()
        phase("mm_near1")
        loaded(loads_a[1])
        loaded(loads_a[2])
        for owner in range(RING * CORES):
            mm_a([(ym, 0), (yp, 1)], owner)
        relays[1].wait_recv()
        relays[2].wait_recv()
        loaded(loads_t[1])
        loaded(loads_t[2])
        for owner in range(RING):
            mm_t([(xm, 0), (xp, 1)], owner)
        phase("mm_near2")
        for n in (1, 3):
            send_t[n].wait_recv()
            relays[3 + n // 2].start()
        for n in (1, 3):
            send_a[n].wait_recv()
        for owner in range(RING * CORES):
            mm_a([(ym, 1), (yp, 0)], owner)
        for n in range(2):
            fwd_t[n].wait_recv()
            relays[5 + n].start()
        relays[3].wait_recv()
        relays[4].wait_recv()
        for owner in range(RING):
            mm_t([(xm, 1), (xp, 0)], owner)
        phase("ag_far")
        fwd_a[0].wait_recv()
        fwd_a[1].wait_recv()
        phase("mm_far")

        loaded(loads_a[3])
        pairs = []
        far_y = [(yf, 0), (yf, 1)]
        for n, i in enumerate((xf, xp, xm, x)):
            mm_a(far_y, i * CORES + other)
            pairs.append(push(PAIR + n, p_a.at[i * CORES + other], d_a.at[i], partner))
            pairs[n].start()
        out_t = ring_scatter(RS_T, lambda i: p_t.at[i], r_t, yp, ym, yf, lambda i: dev(i, x, k))
        out_a = ring_scatter(RS_A, lambda i: p_a.at[i * CORES + k], r_a, xp, xm, xf, lambda i: dev(y, i, k))
        for i in (xf, xp, xm, x):
            mm_a(far_y, i * CORES + k)
        relays[5].wait_recv()
        relays[6].wait_recv()
        loaded(loads_t[3])
        for n, (iy, ix) in enumerate(((yf, xf), (yp, xp), (ym, xm), (y, x))):
            mm_t([(xf, 0), (xf, 1)], iy)
            for q in ((0, 1), (2,), (3,), ())[n]:
                out_t[q].start()
            pairs[n].wait_recv()
            p_a[ix * CORES + k] = p_a[ix * CORES + k] + d_a[ix]
            for q in ((0, 1), (2,), (3,), ())[n]:
                out_a[q].start()
        phase("rs_mid")

        @pl.when(p == SWEEPS)
        def _():
            @pl.when(leaves)
            def _():
                keep_left.wait()
                keep_right.wait()

            @pl.when(stays)
            def _():
                x_move[...] = y_keep[...]

            for op in range(2):
                for q in range(2):
                    x_move[op] = dot_f32(x_move[op], linv[q, op], NT)
            out_right.start()
            y_keep[0] = ycur[0]
            out_left.start()

        ht = width // 2
        out_t[0].wait_recv()
        p_t[yp, 0:ht] = p_t[yp, 0:ht] + r_t[0]
        out_t[4].start()
        out_t[1].wait_recv()
        p_t[ym, ht:width] = p_t[ym, ht:width] + r_t[1]
        out_t[5].start()
        out_a[0].wait_recv()
        kp, km, kk = xp * CORES + k, xm * CORES + k, x * CORES + k
        p_a[kp, 0:hsub] = p_a[kp, 0:hsub] + r_a[0]
        out_a[4].start()
        out_a[1].wait_recv()
        p_a[km, hsub:sub] = p_a[km, hsub:sub] + r_a[1]
        out_a[5].start()
        phase("rs_end")
        for n in (2, 3, 4, 5):
            out_t[n].wait_recv()
            out_a[n].wait_recv()
        phase("rs_sum")
        ycur[t, :, 0:ht] = (p_t[y, 0:ht] + r_t[3] + r_t[4]).T
        ycur[t, :, ht:width] = (p_t[y, ht:width] + r_t[2] + r_t[5]).T
        ycur[a, 0:hsub] = p_a[kk, 0:hsub] + r_a[3] + r_a[4]
        ycur[a, hsub:sub] = p_a[kk, hsub:sub] + r_a[2] + r_a[5]
        phase("rs_drain")
        for copy in send_t + fwd_t + send_a + fwd_a + relays + pairs + out_t + out_a:
            copy.wait_send()
        phase()

    def all_reduce(rows, local):
        piece = rows // nchips
        phase("ar_pair")
        local(other)
        pair = push(GRAM_PAIR, g_loc.at[other, pl.ds(0, rows)], g_pair.at[pl.ds(0, rows)], partner)
        pair.start()
        local(k)
        pair.wait_recv()
        g_sum[0:rows] = g_loc[k, 0:rows] + g_pair[0:rows]

        def chunk(ref, q):
            return ref.at[pl.ds(pl.multiple_of(q * piece, GROUP), piece)]

        def chips():
            for o in range(1, nchips):
                to_y, to_x = lax.rem(y + o // RING, RING), lax.rem(x + o % RING, RING)
                yield o, to_y * RING + to_x, dev(to_y, to_x, k)

        phase("ar_rs")
        mine = y * RING + x
        for o, q, to in chips():
            push(GRAM_RS, chunk(g_sum, q), chunk(g_in, o - 1), to).start()
        others = pl.ds(0, (nchips - 1) * piece)
        pltpu.make_async_copy(g_in.at[others], g_in.at[others], recv.at[GRAM_RS]).wait()
        phase("ar_ag")
        total = chunk(g_sum, mine)[...]
        for o in range(1, nchips):
            total = total + g_in[(o - 1) * piece : o * piece]
        chunk(g_all, mine)[...] = total / total_rows
        for o, q, to in chips():
            push(GRAM_AG, chunk(g_all, mine), chunk(g_all, mine), to).start()
        pltpu.make_async_copy(g_in.at[others], g_in.at[others], recv.at[GRAM_AG]).wait()
        phase("ar_drain")
        pair.wait_send()
        for i in (GRAM_RS, GRAM_AG):
            pltpu.make_async_copy(g_in.at[others], g_in.at[others], send.at[i]).wait()
        phase()

    def gram_blocks(op, dot):
        lo, hi = ycur[op, :, 0:tile], ycur[op, :, tile:width]
        g_loc[op, 0:tile] = dot(lo, lo)
        g_loc[op, tile : 2 * tile] = dot(lo, hi)
        g_loc[op, 2 * tile : 3 * tile] = dot(hi, hi)

    def half_dot(u, v):
        return lax.dot_general(u.astype(BF16), v.astype(BF16), TN, preferred_element_type=F32)

    def full_dot(u, v):
        return dot_f32(u, v, TN)

    def normalize(p, q):
        def local(op):
            @pl.when(q == 0)
            def _():
                gram_blocks(op, half_dot)

            @pl.when(q == 1)
            def _():
                gram_blocks(op, full_dot)

        all_reduce(3 * tile, local)
        last = p == SWEEPS - 1

        @pl.when(jnp.logical_and(last, q == 0))
        def _():
            y_keep[...] = ycur[...]

            @pl.when(leaves)
            def _():
                keep_right.start()

        @pl.when(jnp.logical_and(jnp.logical_and(last, q == 1), leaves))
        def _():
            keep_left.start()

        phase("chol")

        def store(first, t, value):
            linv[q, k, pl.ds(first, GROUP), t * tile : (t + 1) * tile] = value

        linv[q, k, 0:tile, tile:width] = jnp.zeros((tile, tile), F32)
        inverse_factor(g_all, work, store)
        phase("mul_own")
        swap = push(LINV, linv.at[q, k], linv.at[q, k], partner)
        swap.start()
        ycur[k] = dot_f32(ycur[k], linv[q, k], NT)
        phase("mul_other")
        swap.wait_recv()
        ycur[other] = dot_f32(ycur[other], linv[q, other], NT)
        swap.wait_send()
        phase()

    def sweep(p, carry):
        apply(p)

        @pl.when(p < SWEEPS)
        def _():
            def one(q, carry):
                normalize(p, q)
                return carry

            lax.fori_loop(0, 2, one, 0)
            phase("next_x")
            nxt = lax.rem(p + 1, 2)
            for h in range(2):
                rows = slice(h * hsub, (h + 1) * hsub)
                ag_t[c, h] = ycur[nxt, rows].T.astype(BF16)
                ag_a[y, h] = ycur[1 - nxt, rows].astype(BF16)
            phase()

        return carry

    lax.fori_loop(0, SWEEPS + 1, sweep, 0)
    corners = ((0, 0), (0, 1), (1, 0), (1, 1))

    def rayleigh(op):
        for n, (i, j) in enumerate(corners):
            xs, zs = slice(i * tile, (i + 1) * tile), slice(j * tile, (j + 1) * tile)
            g_loc[op, n * tile : (n + 1) * tile] = dot_f32(x_move[op, :, xs], ycur[op, :, zs], TN)

    all_reduce(4 * tile, rayleigh)
    phase("h_swap")
    swap = push(LINV, g_all, h_all, partner)
    swap.start()
    swap.wait()
    for n, (i, j) in enumerate(corners):
        rows, at = slice(n * tile, (n + 1) * tile), (slice(i * tile, (i + 1) * tile), slice(j * tile, (j + 1) * tile))
        for op in range(2):
            h_out[(op, *at)] = jnp.where(k == op, g_all[rows], h_all[rows])
    out_left.wait()
    out_right.wait()
    phase()


def hand_over(x_ref, h_ref, left_x, left_h, right_x, right_h):
    left_x[...] = x_ref[0]
    left_h[...] = h_ref[0]
    right_x[...] = x_ref[1]
    right_h[...] = h_ref[1]


def solution(mesh):
    nrow, ncol = mesh.shape["row"], mesh.shape["col"]
    assert nrow == RING and ncol == RING * CORES

    def local_program(left_op, left_start, right_op, right_start):
        rows, cols = left_op.shape
        sub, width = left_start.shape
        tile = width // 2
        vmem = pltpu.VMEM
        dma = pltpu.SemaphoreType.DMA
        basis, ray = jax.ShapeDtypeStruct((sub, width), F32), jax.ShapeDtypeStruct((width, width), F32)
        both_x, both_h = pl.pallas_call(
            functools.partial(kernel, (nrow, ncol, rows * nrow)),
            out_shape=[jax.ShapeDtypeStruct((2, sub, width), F32), jax.ShapeDtypeStruct((2, width, width), F32)],
            in_specs=[pl.BlockSpec(memory_space=pl.ANY)] * 4,
            out_specs=[pl.BlockSpec(memory_space=pl.ANY), pl.BlockSpec(memory_space=vmem)],
            scratch_shapes=[
                vmem((2, rows, cols), BF16),
                vmem((2, sub, width), F32),
                vmem((ncol, 2, width, sub // 2), BF16),
                vmem((nrow, 2, sub // 2, width), BF16),
                vmem((nrow, width, sub), F32),
                vmem((ncol, sub, width), F32),
                vmem((RING, sub, width), F32),
                vmem((6, width // 2, sub), F32),
                vmem((6, sub // 2, width), F32),
                vmem((sub, width), BF16),
                vmem((2, sub, width), F32),
                vmem((2, sub, width), F32),
                vmem((2, 4 * tile, tile), F32),
                vmem((4 * tile, tile), F32),
                vmem((4 * tile, tile), F32),
                vmem((4 * tile, tile), F32),
                vmem((4 * tile, tile), F32),
                vmem((4 * tile, tile), F32),
                vmem((width, 2 * width), F32),
                vmem((2, 2, width, width), F32),
                dma((COPIES,)),
                dma((COPIES,)),
                dma((10,)),
            ],
            compiler_params=pltpu.CompilerParams(collective_id=0, has_side_effects=True, vmem_limit_bytes=VMEM_BYTES),
            name="subspace",
        )(left_op, left_start, right_op, right_start)
        whole = pl.BlockSpec(memory_space=vmem)
        return pl.pallas_call(
            hand_over, out_shape=[basis, ray, basis, ray], in_specs=[whole] * 2, out_specs=[whole] * 4, name="hand_over"
        )(both_x, both_h)

    op_spec = P(("batch", "row"), "col")
    vec_spec = P(("batch", "row", "col"), None)
    small_spec = P("batch", None)
    return jax.shard_map(
        local_program,
        mesh=mesh,
        in_specs=(op_spec, vec_spec, op_spec, vec_spec),
        out_specs=(vec_spec, small_spec, vec_spec, small_spec),
        check_vma=False,
    )
```

time: 447 us -> 406 us (0.908)
  Pallas kernels: 439 us -> 405 us
  local copies, waits for them, and re-layouts: 7.07 us -> 0 us
    pallas_call x1, Pallas kernels: 439 us -> 403 us  [local_program(): pl.pallas_call(functools.partial(kernel, (nrow, ncol, rows * nrow)), out_...]
    unnamed x4 -> x0, local copies, waits for them, and re-layouts: 7.07 us -> none
where the time goes in v2:
time: 406 us
  Pallas kernels  405 us (100%)
    pallas_call x1, Pallas kernels, local_program(): pl.pallas_call(functools.partial(kernel, (nrow, ncol, rows * nrow)), out_...  403 us

profile of v2, /device:TPU:97, one launch (start us, length us, event | category | flops | bytes accessed | tf_op | source)
XLA Modules:
  0.0 406.0 jit_solution(2747551288020162309)
XLA Ops:
  0.6 402.9 %subspace.1 = (f32[2,512,256]{2,1,0:T(8,128)}, f32[2,256,256]{2,1,0:T(8,128)}) custom-call(bf16[4096,2048]{1,0:T(8,128)(2,1)} %left_op.1, f32[512,256]{1,0:T(8,128)} %left_start.1, bf16[4096,2048]{1,0:T(8,128)(2,1)} %right_op.1, f32[512,256]{1,0:T(8,128)} %right_start.1), custom_call_target="tpu_custom_call" | custom-call | tf_op jit(solution)/shard_map/subspace/pallas_call | solution.py:575
  403.5 2.5 hand_over.1
